TPU v7x, 256 devices: a 8x8x2 block of a 8x8x16 slice. The times are simulated.
256 devices in a mesh: groups: 2 (over z), section: 2 (over core), mesh: 64 (over x, y).
Axes of the slice: x: 8, y: 8, z: 2, core: 2. Of those that a mesh axis runs over, the one named last changes fastest.
The devices are a block of a 8x8x16 slice.
Arguments:
- inputs: bfloat16 [4, 128, 8192], P('groups', None, 'mesh'), parts along dimension 0, may hold values from -12 to 12
- segments: int32 [4, 128], P('groups'), parts along dimension 0, may hold values from 0 to 3, never falling along the last dimension, each value on 1 to 64 neighbouring positions
- gains: bfloat16 [2, 1, 8192], P('section'), may hold values from 0.25 to 1.75
- w_query: bfloat16 [2, 1, 8192, 8192], P('section', None, None, 'mesh'), may hold values from -1.3258252 to 1.3258252
- w_keyval: bfloat16 [2, 1, 8192, 2048], P('section', None, None, 'mesh'), may hold values from -0.055242717 to 0.055242717
- w_output: bfloat16 [2, 1, 8192, 8192], P('section', None, None, 'mesh'), may hold values from -0.0625 to 0.0625
Outputs:
- section_outputs: bfloat16 [2, 4, 128, 8192], P('section', 'groups', None, 'mesh'), parts along dimension 1
There are 2 independent parts, one for each index of `groups`. A program takes and returns all parts, laid end to end along the dimension named above; an argument that names none is the same for every part. Nothing has to cross between parts.
Inputs may be any that keep to these rules, and one draw needn't show every extreme that they name: `segments`: along each micro-batch the document ids never fall; each document spans 1 to 64 positions.
All inputs are finite; a program needn't handle non-finite values.
Results may differ from a plain program's by a relative error of at most 0.0052.
Values may be sent and summed in bfloat16 or wider, within the bound.
No kernel may reach another device: no remote copies, remote signals or barrier semaphores. Data moves between devices by JAX's collectives and lax.ppermute only.
A program may use at most 64 MiB of HBM per device.

v0:
```python
import jax
import jax.numpy as jnp
from jax import lax
from jax.sharding import Mesh
from jax.sharding import PartitionSpec as P

HD = 128
GROUP = 8
MESH = ("mesh_0", "mesh_1")
norm_epsilon = 1e-05
rope_theta = 500000.0


def joined_along(parts, dim):
    lengths = list(parts.shape[1:])
    lengths[dim] *= parts.shape[0]
    return jnp.moveaxis(parts, 0, dim).reshape(lengths)


def gather_in_order(x, axes, sequence):
    parts = x[None]
    for k in sequence:
        parts = lax.all_gather(parts, axes[k], axis=0, tiled=True)
    block = [lax.axis_size(axes[k]) for k in reversed(sequence)]
    parts = parts.reshape(*block, *x.shape)
    turned = sorted(range(len(sequence)), key=lambda place: sequence[len(sequence) - 1 - place])
    return parts.transpose(*turned, *range(len(sequence), parts.ndim)).reshape(-1, *x.shape)


def whole_of(x, axes, sequence, dim):
    return joined_along(gather_in_order(x, axes, sequence), dim)


def partner_2(x, axis, distance):
    return lax.ppermute(x, axis, [(i, i ^ 1 << distance) for i in range(lax.axis_size(axis))])


def from_behind(block, axis, distance):
    devices = range(lax.axis_size(axis))
    route = [(i - distance, i) for i in devices if i - distance in devices]
    return lax.ppermute(block, axis, route)


def position_tables(segment_row):
    row_length = segment_row.shape[0]
    indices = jnp.arange(row_length, dtype=jnp.int32)
    doc_starts = jnp.concatenate([jnp.ones((1,), dtype=bool), segment_row[1:] != segment_row[:-1]])
    first_index = lax.cummax(jnp.where(doc_starts, indices, jnp.zeros_like(indices)), axis=0)
    positions = (indices - first_index).astype(jnp.float32)
    half_width = HD // 2
    freqs = rope_theta ** (-(2.0 * jnp.arange(half_width, dtype=jnp.float32)) / HD)
    angles = positions[:, None] * freqs[None, :]
    cosine_table = jnp.concatenate([jnp.cos(angles), jnp.cos(angles)], axis=1)
    sine_table = jnp.concatenate([jnp.sin(angles), jnp.sin(angles)], axis=1)
    allowed = (indices[None, :] <= indices[:, None]) & (
        segment_row[None, :] == segment_row[:, None]
    )
    return (cosine_table, sine_table, allowed)


def rotate(values, cosine_table, sine_table):
    half_width = values.shape[-1] // 2
    turned = jnp.concatenate([-values[..., half_width:], values[..., :half_width]], axis=-1)
    return values * cosine_table + turned * sine_table


def softmax_weights(scores, allowed):
    masked = jnp.where(allowed, scores, -1e30)
    highest = jnp.max(masked, axis=-1, keepdims=True)
    raised = jnp.exp(masked - highest)
    return (raised / jnp.sum(raised, axis=-1, keepdims=True)).astype(jnp.bfloat16)


def apply_layer(
    activations,
    gain_row,
    query_weight,
    keyval_weight,
    output_weight,
    cosine_table,
    sine_table,
    allowed,
    mesh_index,
):
    floats = activations.astype(jnp.float32)
    gathered = whole_of(activations, MESH, (0, 1), 1)
    whole_floats = gathered.astype(jnp.float32)
    scale = lax.rsqrt(jnp.mean(whole_floats * whole_floats, axis=1, keepdims=True) + norm_epsilon)
    normed = (whole_floats * scale * gain_row.astype(jnp.float32)).astype(jnp.bfloat16)
    query_raw = jnp.dot(normed, query_weight, preferred_element_type=jnp.float32)
    keyval_raw = jnp.dot(normed, keyval_weight, preferred_element_type=jnp.float32)
    query = rotate(query_raw, cosine_table, sine_table).astype(jnp.bfloat16)
    keyval_part = keyval_raw.astype(jnp.bfloat16)
    for bit_index in range(GROUP.bit_length() - 1):
        partner = partner_2(keyval_part, MESH, bit_index)
        upper_half = mesh_index // (1 << bit_index) % 2 == 1
        keyval_part = jnp.where(
            upper_half,
            jnp.concatenate([partner, keyval_part], axis=1),
            jnp.concatenate([keyval_part, partner], axis=1),
        )
    keys = rotate(keyval_part[:, :HD].astype(jnp.float32), cosine_table, sine_table).astype(
        jnp.bfloat16
    )
    values = keyval_part[:, HD:]
    scores = jnp.dot(query, keys.T, preferred_element_type=jnp.float32) * HD ** (-0.5)
    probs = softmax_weights(scores, allowed)
    attended = jnp.dot(probs, values, preferred_element_type=jnp.float32).astype(jnp.bfloat16)
    mixed = jnp.dot(
        whole_of(attended, MESH, (0, 1), 1), output_weight, preferred_element_type=jnp.float32
    )
    return (floats + mixed).astype(jnp.bfloat16)


def shards(inputs, segments, gains, w_query, w_keyval, w_output):
    micro_count, row_count, local_cols = inputs.shape
    section_count = lax.axis_size("section")
    section_index = lax.axis_index("section")
    mesh_index = lax.axis_index(MESH)
    cosine_list, sine_list, allowed_list = ([], [], [])
    for micro_index in range(micro_count):
        cosine_table, sine_table, allowed = position_tables(segments[micro_index])
        cosine_list.append(cosine_table)
        sine_list.append(sine_table)
        allowed_list.append(allowed)
    cosine_all = jnp.stack(cosine_list)
    sine_all = jnp.stack(sine_list)
    allowed_all = jnp.stack(allowed_list)
    step_count = micro_count + section_count - 1
    received = jnp.zeros((row_count, local_cols), jnp.bfloat16)
    results = []
    for section_step in range(step_count):
        feed_slot = min(section_step, micro_count - 1)
        micro_here = jnp.clip(section_step - section_index, 0, micro_count - 1)
        cosine_table = lax.dynamic_index_in_dim(cosine_all, micro_here, 0, keepdims=False)
        sine_table = lax.dynamic_index_in_dim(sine_all, micro_here, 0, keepdims=False)
        allowed = lax.dynamic_index_in_dim(allowed_all, micro_here, 0, keepdims=False)
        current = jnp.where(section_index == 0, inputs[feed_slot], received)
        current = apply_layer(
            current,
            gains[0, 0],
            w_query[0, 0],
            w_keyval[0, 0],
            w_output[0, 0],
            cosine_table,
            sine_table,
            allowed,
            mesh_index,
        )
        results.append(current)
        if section_step + 1 < step_count:
            received = from_behind(current, "section", 1)
    stacked = jnp.stack(results)
    chosen = lax.dynamic_slice_in_dim(stacked, section_index, micro_count, 0)
    return chosen[None]


def solution(mesh):
    finer = Mesh(
        mesh.devices.reshape(mesh.shape["groups"], mesh.shape["section"], 8, 8),
        ("groups", "section", "mesh_0", "mesh_1"),
    )
    in_specs = (
        P("groups", None, MESH),
        P("groups", None),
        P("section", None, None),
        P("section", None, None, MESH),
        P("section", None, None, MESH),
        P("section", None, None, MESH),
    )
    out_specs = P("section", "groups", None, MESH)
    return jax.shard_map(
        shards, mesh=finer, in_specs=in_specs, out_specs=out_specs, check_vma=False
    )
```

profile of v0, /device:TPU:514, one launch (start us, length us, event | category | flops | bytes accessed | tf_op | source)
XLA Modules:
  0.0 562.5 jit_solution(12271159927433915738)
XLA Ops:
  7.5 43.0 %all_gather.36 = bf16[8,128,128]{2,1,0:T(8,128)(2,1)} all-gather(bf16[1,128,128]{2,1,0:T(8,128)(2,1)S(1)} %slice_select_fusion), channel_id=1, replica_groups=mesh['groups'=2,'section'=2,'mesh_0'=8,'mesh_1'=8] {'mesh_0'}, dimensions={0}, use_global_device_ids=true | all-gather | bytes 294912 | tf_op jit(solution)/shard_map/all_gather | solution.py:23
  54.5 40.1 %all-gather.12.cloned.1.call-done = bf16[64,128,128]{2,1,0:T(8,128)(2,1)} async-done(((bf16[8,128,128]{2,1,0:T(8,128)(2,1)}), bf16[64,128,128]{2,1,0:T(8,128)(2,1)}) %all-gather.12.cloned.1.call-update) | async-done | bytes 2097168 | tf_op jit(solution)/shard_map/all_gather | solution.py:23
  94.5 2.1 convert_bitcast_fusion.2
  97.5 2.2 fusion.8
  99.7 4.1 copy.46
  103.9 2.0 convolution_convert_fusion.5
  107.4 2.3 collective-permute-done
  109.7 1.6 collective-permute-start.1
  111.3 2.4 fusion.19
  114.4 3.2 collective-permute-start.2
  117.7 4.7 collective-permute-done.2
  122.9 27.0 %all-gather = bf16[1024,128]{1,0:T(8,128)(2,1)} all-gather(bf16[128,128]{1,0:T(8,128)(2,1)S(1)} %convolution_convert_fusion.2), channel_id=2, replica_groups=mesh['groups'=2,'section'=2,'mesh_0'=8,'mesh_1'=8] {'mesh_0'}, dimensions={0}, use_global_device_ids=true | all-gather | bytes 294912 | tf_op jit(solution)/shard_map/all_gather | solution.py:23
  150.0 41.0 %all-gather.14.cloned.1.call-done = bf16[64,128,128]{2,1,0:T(8,128)(2,1)} async-done(((bf16[8,128,128]{2,1,0:T(8,128)(2,1)}), bf16[64,128,128]{2,1,0:T(8,128)(2,1)}) %all-gather.14.cloned.1.call-update) | async-done | bytes 2097168 | tf_op jit(solution)/shard_map/all_gather | solution.py:23
  191.0 3.1 copy.49
  194.1 4.1 copy.50
  198.2 3.0 fusion.27
  203.4 27.0 %all-gather.1 = bf16[1024,128]{1,0:T(8,128)(2,1)} all-gather(bf16[128,128]{1,0:T(8,128)(2,1)S(1)} %bitcast_select_fusion.1), channel_id=3, replica_groups=mesh['groups'=2,'section'=2,'mesh_0'=8,'mesh_1'=8] {'mesh_0'}, dimensions={0}, use_global_device_ids=true | all-gather | bytes 294912 | tf_op jit(solution)/shard_map/all_gather | solution.py:23
  230.7 40.7 %all-gather.16.cloned.1.call-done = bf16[64,128,128]{2,1,0:T(8,128)(2,1)} async-done(((bf16[8,128,128]{2,1,0:T(8,128)(2,1)}), bf16[64,128,128]{2,1,0:T(8,128)(2,1)}) %all-gather.16.cloned.1.call-update) | async-done | bytes 2097168 | tf_op jit(solution)/shard_map/all_gather | solution.py:23
  271.4 2.1 convert_bitcast_fusion.1
  274.4 2.2 fusion.5
  276.6 4.1 copy.52
  280.7 2.0 convolution_convert_fusion.4
  284.2 2.3 collective-permute-done.4
  286.5 1.6 collective-permute-start.5
  288.1 2.4 fusion.17
  291.3 3.2 collective-permute-start.6
  294.5 4.7 collective-permute-done.6
  299.7 27.0 %all-gather.2 = bf16[1024,128]{1,0:T(8,128)(2,1)} all-gather(bf16[128,128]{1,0:T(8,128)(2,1)S(1)} %convolution_convert_fusion.1), channel_id=4, replica_groups=mesh['groups'=2,'section'=2,'mesh_0'=8,'mesh_1'=8] {'mesh_0'}, dimensions={0}, use_global_device_ids=true | all-gather | bytes 294912 | tf_op jit(solution)/shard_map/all_gather | solution.py:23
  326.8 41.0 %all-gather.18.cloned.1.call-done = bf16[64,128,128]{2,1,0:T(8,128)(2,1)} async-done(((bf16[8,128,128]{2,1,0:T(8,128)(2,1)}), bf16[64,128,128]{2,1,0:T(8,128)(2,1)}) %all-gather.18.cloned.1.call-update) | async-done | bytes 2097168 | tf_op jit(solution)/shard_map/all_gather | solution.py:23
  367.8 3.1 copy.53
  371.0 4.1 copy.54
  375.0 3.0 add_convert_fusion.1
  380.2 27.0 %all-gather.3 = bf16[1024,128]{1,0:T(8,128)(2,1)} all-gather(bf16[128,128]{1,0:T(8,128)(2,1)S(1)} %bitcast_select_fusion), channel_id=5, replica_groups=mesh['groups'=2,'section'=2,'mesh_0'=8,'mesh_1'=8] {'mesh_0'}, dimensions={0}, use_global_device_ids=true | all-gather | bytes 294912 | tf_op jit(solution)/shard_map/all_gather | solution.py:23
  407.3 40.9 %all-gather.20.cloned.1.call-done = bf16[64,128,128]{2,1,0:T(8,128)(2,1)} async-done(((bf16[8,128,128]{2,1,0:T(8,128)(2,1)}), bf16[64,128,128]{2,1,0:T(8,128)(2,1)}) %all-gather.20.cloned.1.call-update) | async-done | bytes 2097168 | tf_op jit(solution)/shard_map/all_gather | solution.py:23
  448.1 2.1 convert_bitcast_fusion
  451.1 2.2 fusion.2
  453.3 4.1 copy.56
  457.4 2.0 convolution_convert_fusion.3
  460.9 2.3 collective-permute-done.8
  463.2 1.8 collective-permute-start.9
  465.0 2.4 fusion.15
  468.2 3.2 collective-permute-start.10
  471.4 4.7 collective-permute-done.10
  476.7 27.0 %all-gather.4 = bf16[1024,128]{1,0:T(8,128)(2,1)} all-gather(bf16[128,128]{1,0:T(8,128)(2,1)S(1)} %convolution_convert_fusion), channel_id=6, replica_groups=mesh['groups'=2,'section'=2,'mesh_0'=8,'mesh_1'=8] {'mesh_0'}, dimensions={0}, use_global_device_ids=true | all-gather | bytes 294912 | tf_op jit(solution)/shard_map/all_gather | solution.py:23
  503.7 41.0 %all-gather.22.cloned.1.call-done = bf16[64,128,128]{2,1,0:T(8,128)(2,1)} async-done(((bf16[8,128,128]{2,1,0:T(8,128)(2,1)}), bf16[64,128,128]{2,1,0:T(8,128)(2,1)}) %all-gather.22.cloned.1.call-update) | async-done | bytes 2097168 | tf_op jit(solution)/shard_map/all_gather | solution.py:23
  544.7 3.1 copy.57
  547.9 4.1 copy.58
  551.9 3.0 fusion.71
  (87 shorter events, 21.7 us)
Async XLA Ops:
  6.5 104.7 %copy-start = (bf16[1,1,8192,128]{3,2,1,0:T(8,128)(2,1)S(1)}, bf16[1,1,8192,128]{3,2,1,0:T(8,128)(2,1)}, u32[]{:S(2)}) copy-start(bf16[1,1,8192,128]{3,2,1,0:T(8,128)(2,1)} %param.9) | copy-start | bytes 6291460
  6.6 88.0 %all-gather.12.cloned.1.call-start = ((), (), s32[]{:S(2)}) async-start(), calls=%async_computation | async-start | bytes 2359296 | tf_op jit(solution)/shard_map/all_gather | solution.py:23
  50.6 140.4 %all-gather.14.cloned.1.call-start = ((), (), s32[]{:S(2)}) async-start(), calls=%async_computation.1 | async-start | bytes 2359296 | tf_op jit(solution)/shard_map/all_gather | solution.py:23
  99.7 4.1 copy-start.1
  105.9 3.8 collective-permute-start
  109.7 4.8 collective-permute-start.1
  114.4 7.9 %collective-permute-start.2 = (bf16[128,128]{0,1:T(8,128)(2,1)S(1)}, bf16[128,128]{0,1:T(8,128)(2,1)S(1)}, u32[]{:S(2)}, u32[]{:S(2)}) collective-permute-start(bf16[128,128]{0,1:T(8,128)(2,1)S(1)} %maximum_select_fusion.3), channel_id=1, source_target_pairs={{0,4},{1,5},{2,6},{3,7},{4,0},{5,1},{6,2},{7,3},{8,12},{9,13},{10,... | collective-permute-start | bytes 98312 | tf_op jit(solution)/shard_map/ppermute | solution.py:35
  150.0 121.4 %all-gather.16.cloned.1.call-start = ((), (), s32[]{:S(2)}) async-start(), calls=%async_computation.2 | async-start | bytes 2359296 | tf_op jit(solution)/shard_map/all_gather | solution.py:23
  198.2 5.2 copy-start.2
  201.2 2.2 collective-permute-start.3
  230.5 137.3 %all-gather.18.cloned.1.call-start = ((), (), s32[]{:S(2)}) async-start(), calls=%async_computation.3 | async-start | bytes 2359296 | tf_op jit(solution)/shard_map/all_gather | solution.py:23
  282.7 3.8 collective-permute-start.4
  286.5 4.8 collective-permute-start.5
  291.3 7.9 %collective-permute-start.6 = (bf16[128,128]{0,1:T(8,128)(2,1)S(1)}, bf16[128,128]{0,1:T(8,128)(2,1)S(1)}, u32[]{:S(2)}, u32[]{:S(2)}) collective-permute-start(bf16[128,128]{0,1:T(8,128)(2,1)S(1)} %maximum_select_fusion.4), channel_id=1, source_target_pairs={{0,4},{1,5},{2,6},{3,7},{4,0},{5,1},{6,2},{7,3},{8,12},{9,13},{10,... | collective-permute-start | bytes 98312 | tf_op jit(solution)/shard_map/ppermute | solution.py:35
  326.8 121.3 %all-gather.20.cloned.1.call-start = ((), (), s32[]{:S(2)}) async-start(), calls=%async_computation.4 | async-start | bytes 2359296 | tf_op jit(solution)/shard_map/all_gather | solution.py:23
  378.0 2.2 collective-permute-start.7
  407.2 137.5 %all-gather.22.cloned.1.call-start = ((), (), s32[]{:S(2)}) async-start(), calls=%async_computation.5 | async-start | bytes 2359296 | tf_op jit(solution)/shard_map/all_gather | solution.py:23
  459.4 3.8 collective-permute-start.8
  463.2 5.0 collective-permute-start.9
  468.2 7.9 %collective-permute-start.10 = (bf16[128,128]{0,1:T(8,128)(2,1)S(1)}, bf16[128,128]{0,1:T(8,128)(2,1)S(1)}, u32[]{:S(2)}, u32[]{:S(2)}) collective-permute-start(bf16[128,128]{0,1:T(8,128)(2,1)S(1)} %maximum_select_fusion.5), channel_id=1, source_target_pairs={{0,4},{1,5},{2,6},{3,7},{4,0},{5,1},{6,2},{7,3},{8,12},{9,13},{10,... | collective-permute-start | bytes 98312 | tf_op jit(solution)/shard_map/ppermute | solution.py:35
Sparse Core Ops, SparseCore 0:
  50.7 43.8 all-gather.11
  150.1 40.8 all-gather.13
  230.6 40.7 all-gather.15
  326.9 40.8 all-gather.17
  407.3 40.7 all-gather.19
  503.8 40.8 all-gather.21
where the time goes:
time: 564 us; the launch traced here: 562 us
  waiting for transfers between devices  270 us (48%)
  blocking collectives  178 us (32%)
  local copies, waits for them, and re-layouts  36.4 us (6%)
  matrix products  23.5 us (4%)
  starting transfers between devices  22.3 us (4%)
  other arithmetic  18.8 us (3%)
  between operations  13.8 us (2%)
    all_gather x6, waiting for transfers between devices, gather_in_order(): parts = lax.all_gather(parts, axes[k], axis=0, tiled=True)  245 us
    all_gather x6, blocking collectives, gather_in_order(): parts = lax.all_gather(parts, axes[k], axis=0, tiled=True)  178 us
    ppermute x9, waiting for transfers between devices, partner_2(): lax.ppermute(x, axis, [(i, i ^ 1 << distance) for i in range(lax.axis_siz...  23.4 us
    ppermute x9, starting transfers between devices, partner_2(): lax.ppermute(x, axis, [(i, i ^ 1 << distance) for i in range(lax.axis_siz...  19.2 us
    convert_element_type x3, local copies, waits for them, and re-layouts, apply_layer(): (whole_floats * scale * gain_row.astype(jnp.float32)).astype(jnp.bfloat16)  12.2 us
    transpose x3, local copies, waits for them, and re-layouts, joined_along(): return jnp.moveaxis(parts, 0, dim).reshape(lengths)  12.2 us
  transfers between devices with their start and end apart: 17, of which 17 were waited for; matrix products, arithmetic and copies ran while one was open for 2% of the time, Pallas kernels for 0%

commit v1 on v0

--- a/solution.py
+++ b/solution.py
@@ -20,7 +20,13 @@
 def gather_in_order(x, axes, sequence):
     parts = x[None]
     for k in sequence:
-        parts = lax.all_gather(parts, axes[k], axis=0, tiled=True)
+        page = axes[k]
+        series = []
+        for _ in range(jax.lax.axis_size(page)):
+            series.append(parts)
+        prior = jnp.stack(series, axis=0)
+        w_next = jax.lax.all_to_all(prior, axis_name=page, split_axis=0, concat_axis=0)
+        parts = jnp.concatenate(w_next, axis=0)
     block = [lax.axis_size(axes[k]) for k in reversed(sequence)]
     parts = parts.reshape(*block, *x.shape)
     turned = sorted(range(len(sequence)), key=lambda place: sequence[len(sequence) - 1 - place])

time: 564 us -> 533 us (0.945)
  waiting for transfers between devices: 270 us -> 129 us
  blocking collectives: 178 us -> 305 us
  between operations: 13.8 us -> 0.4 us
    all_to_all x0 -> x10, blocking collectives: none -> 305 us  [gather_in_order(): jax.lax.all_to_all(prior, axis_name=page, split_axis=0, concat_axis=0)]
    all_gather x6 -> x0, waiting for transfers between devices: 245 us -> none  [gather_in_order(): parts = lax.all_gather(parts, axes[k], axis=0, tiled=True)]
    all_gather x6 -> x0, blocking collectives: 178 us -> none  [gather_in_order(): parts = lax.all_gather(parts, axes[k], axis=0, tiled=True)]
    all_to_all x0 -> x2, waiting for transfers between devices: none -> 89.8 us  [gather_in_order(): jax.lax.all_to_all(prior, axis_name=page, split_axis=0, concat_axis=0)]
    ppermute x9, waiting for transfers between devices: 23.4 us -> 37.9 us  [partner_2(): lax.ppermute(x, axis, [(i, i ^ 1 << distance) for i in range(lax.axis_siz...]
    ppermute x9, starting transfers between devices: 19.2 us -> 5.1 us  [partner_2(): lax.ppermute(x, axis, [(i, i ^ 1 << distance) for i in range(lax.axis_siz...]
    transpose x3 -> x0, local copies, waits for them, and re-layouts: 9.44 us -> none  [gather_in_order(): parts.transpose(*turned, *range(len(sequence), parts.ndim))]
    all_to_all x0 -> x2, starting transfers between devices: none -> 9.17 us  [gather_in_order(): jax.lax.all_to_all(prior, axis_name=page, split_axis=0, concat_axis=0)]
  transfers between devices with their start and end apart: 17 -> 13, of which waited for: 17 -> 13; matrix products, arithmetic and copies ran while one was open for 2% -> 2% of each run, Pallas kernels for 0% -> 0%
where the time goes in v1:
time: 533 us; the launch traced here: 528 us
  blocking collectives  305 us (57%)
  waiting for transfers between devices  129 us (24%)
  local copies, waits for them, and re-layouts  37.7 us (7%)
  matrix products  23.5 us (4%)
  starting transfers between devices  16.9 us (3%)
  other arithmetic  15.3 us (3%)
    all_to_all x10, blocking collectives, gather_in_order(): jax.lax.all_to_all(prior, axis_name=page, split_axis=0, concat_axis=0)  305 us
    all_to_all x2, waiting for transfers between devices, gather_in_order(): jax.lax.all_to_all(prior, axis_name=page, split_axis=0, concat_axis=0)  89.8 us
    ppermute x9, waiting for transfers between devices, partner_2(): lax.ppermute(x, axis, [(i, i ^ 1 << distance) for i in range(lax.axis_siz...  37.9 us
    convert_element_type x3, local copies, waits for them, and re-layouts, apply_layer(): (whole_floats * scale * gain_row.astype(jnp.float32)).astype(jnp.bfloat16)  12.3 us
    transpose x3, local copies, waits for them, and re-layouts, joined_along(): return jnp.moveaxis(parts, 0, dim).reshape(lengths)  12.3 us
  transfers between devices with their start and end apart: 13, of which 13 were waited for; matrix products, arithmetic and copies ran while one was open for 2% of the time, Pallas kernels for 0%

profile of v1, /device:TPU:514, one launch (start us, length us, event | category | flops | bytes accessed | tf_op | source)
XLA Modules:
  0.0 528.2 jit_solution(13742891630461313655)
XLA Ops:
  1.0 30.9 %all_to_all.60 = bf16[8,1,128,128]{3,2,1,0:T(8,128)(2,1)S(1)} all-to-all(bf16[8,1,128,128]{3,2,1,0:T(8,128)(2,1)S(1)} %stack.72), channel_id=1, replica_groups=mesh['groups'=2,'section'=2,'mesh_0'=8,'mesh_1'=8] {'mesh_0'}, dimensions={0} | all-to-all | bytes 524288 | tf_op jit(solution)/shard_map/all_to_all | solution.py:28
  31.8 1.8 stack.73
  33.7 4.7 all-to-all-start.1
  39.8 43.1 %all-to-all-done.1 = bf16[8,8,128,128]{3,2,1,0:T(8,128)(2,1)} async-done(((bf16[8,8,128,128]{3,2,1,0:T(8,128)(2,1)}), bf16[8,8,128,128]{3,2,1,0:T(8,128)(2,1)}, u32[]{:S(2)}, u32[]{:S(2)}) %all-to-all-start.1) | async-done | bytes 2097184 | tf_op jit(solution)/shard_map/all_to_all | solution.py:28
  82.9 2.1 fusion.6
  85.0 3.8 fusion.8
  88.9 4.2 copy.18
  93.0 2.0 convolution_convert_fusion.5
  95.7 3.1 collective-permute-done
  99.3 2.4 fusion.19
  101.7 2.1 collective-permute-done.1
  104.4 7.3 %collective-permute-done.2 = bf16[128,128]{0,1:T(8,128)(2,1)S(1)} collective-permute-done((bf16[128,128]{0,1:T(8,128)(2,1)S(1)}, bf16[128,128]{0,1:T(8,128)(2,1)S(1)}, u32[]{:S(2)}, u32[]{:S(2)}) %collective-permute-start.2) | collective-permute-done | bytes 32800 | tf_op jit(solution)/shard_map/ppermute | solution.py:41
  112.3 14.5 %all_to_all.61 = bf16[8,1,128,128]{3,2,1,0:T(8,128)(2,1)S(1)} all-to-all(bf16[8,1,128,128]{3,2,1,0:T(8,128)(2,1)S(1)} %stack.80), channel_id=1, replica_groups=mesh['groups'=2,'section'=2,'mesh_0'=8,'mesh_1'=8] {'mesh_0'}, dimensions={0} | all-to-all | bytes 524288 | tf_op jit(solution)/shard_map/all_to_all | solution.py:28
  127.2 46.4 %all_to_all.62 = bf16[8,8,128,128]{3,2,1,0:T(8,128)(2,1)S(1)} all-to-all(bf16[8,8,128,128]{3,2,1,0:T(8,128)(2,1)S(1)} %stack.81), channel_id=1, replica_groups=mesh['groups'=2,'section'=2,'mesh_0'=8,'mesh_1'=8] {'mesh_1'}, dimensions={0} | all-to-all | bytes 4194304 | tf_op jit(solution)/shard_map/all_to_all | solution.py:28
  173.7 1.5 copy.21
  175.2 4.1 copy.22
  179.3 3.0 fusion.27
  182.3 1.3 collective-permute-start.3
  184.5 15.5 %all_to_all.63 = bf16[8,1,128,128]{3,2,1,0:T(8,128)(2,1)S(1)} all-to-all(bf16[8,1,128,128]{3,2,1,0:T(8,128)(2,1)S(1)} %stack.83), channel_id=1, replica_groups=mesh['groups'=2,'section'=2,'mesh_0'=8,'mesh_1'=8] {'mesh_0'}, dimensions={0} | all-to-all | bytes 524288 | tf_op jit(solution)/shard_map/all_to_all | solution.py:28
  200.5 52.1 %all_to_all.64 = bf16[8,8,128,128]{3,2,1,0:T(8,128)(2,1)S(1)} all-to-all(bf16[8,8,128,128]{3,2,1,0:T(8,128)(2,1)S(1)} %stack.84), channel_id=1, replica_groups=mesh['groups'=2,'section'=2,'mesh_0'=8,'mesh_1'=8] {'mesh_1'}, dimensions={0} | all-to-all | bytes 4194304 | tf_op jit(solution)/shard_map/all_to_all | solution.py:28
  253.9 2.2 fusion.5
  256.1 4.1 copy.24
  260.2 2.0 convolution_convert_fusion.4
  263.2 3.1 collective-permute-done.4
  266.6 2.4 fusion.17
  269.0 2.2 collective-permute-done.5
  271.7 7.4 %collective-permute-done.6 = bf16[128,128]{0,1:T(8,128)(2,1)S(1)} collective-permute-done((bf16[128,128]{0,1:T(8,128)(2,1)S(1)}, bf16[128,128]{0,1:T(8,128)(2,1)S(1)}, u32[]{:S(2)}, u32[]{:S(2)}) %collective-permute-start.6) | collective-permute-done | bytes 32800 | tf_op jit(solution)/shard_map/ppermute | solution.py:41
  279.7 14.5 %all_to_all.65 = bf16[8,1,128,128]{3,2,1,0:T(8,128)(2,1)S(1)} all-to-all(bf16[8,1,128,128]{3,2,1,0:T(8,128)(2,1)S(1)} %stack.85), channel_id=1, replica_groups=mesh['groups'=2,'section'=2,'mesh_0'=8,'mesh_1'=8] {'mesh_0'}, dimensions={0} | all-to-all | bytes 524288 | tf_op jit(solution)/shard_map/all_to_all | solution.py:28
  294.7 49.2 %all_to_all.66 = bf16[8,8,128,128]{3,2,1,0:T(8,128)(2,1)S(1)} all-to-all(bf16[8,8,128,128]{3,2,1,0:T(8,128)(2,1)S(1)} %stack.86), channel_id=1, replica_groups=mesh['groups'=2,'section'=2,'mesh_0'=8,'mesh_1'=8] {'mesh_1'}, dimensions={0} | all-to-all | bytes 4194304 | tf_op jit(solution)/shard_map/all_to_all | solution.py:28
  344.0 1.5 copy.25
  345.5 4.1 copy.26
  349.5 3.0 add_convert_fusion.1
  354.7 15.5 %all_to_all.67 = bf16[8,1,128,128]{3,2,1,0:T(8,128)(2,1)S(1)} all-to-all(bf16[8,1,128,128]{3,2,1,0:T(8,128)(2,1)S(1)} %stack.88), channel_id=1, replica_groups=mesh['groups'=2,'section'=2,'mesh_0'=8,'mesh_1'=8] {'mesh_0'}, dimensions={0} | all-to-all | bytes 524288 | tf_op jit(solution)/shard_map/all_to_all | solution.py:28
  370.7 52.1 %all_to_all.68 = bf16[8,8,128,128]{3,2,1,0:T(8,128)(2,1)S(1)} all-to-all(bf16[8,8,128,128]{3,2,1,0:T(8,128)(2,1)S(1)} %stack.89), channel_id=1, replica_groups=mesh['groups'=2,'section'=2,'mesh_0'=8,'mesh_1'=8] {'mesh_1'}, dimensions={0} | all-to-all | bytes 4194304 | tf_op jit(solution)/shard_map/all_to_all | solution.py:28
  424.2 2.2 fusion.2
  426.4 4.1 copy.28
  430.5 2.0 convolution_convert_fusion.3
  433.2 3.1 collective-permute-done.8
  436.7 2.4 fusion.15
  439.0 2.2 collective-permute-done.9
  441.7 7.4 %collective-permute-done.10 = bf16[128,128]{0,1:T(8,128)(2,1)S(1)} collective-permute-done((bf16[128,128]{0,1:T(8,128)(2,1)S(1)}, bf16[128,128]{0,1:T(8,128)(2,1)S(1)}, u32[]{:S(2)}, u32[]{:S(2)}) %collective-permute-start.10) | collective-permute-done | bytes 32800 | tf_op jit(solution)/shard_map/ppermute | solution.py:41
  449.8 14.5 %all_to_all.69 = bf16[8,1,128,128]{3,2,1,0:T(8,128)(2,1)S(1)} all-to-all(bf16[8,1,128,128]{3,2,1,0:T(8,128)(2,1)S(1)} %stack.90), channel_id=1, replica_groups=mesh['groups'=2,'section'=2,'mesh_0'=8,'mesh_1'=8] {'mesh_0'}, dimensions={0} | all-to-all | bytes 524288 | tf_op jit(solution)/shard_map/all_to_all | solution.py:28
  464.3 1.8 stack.91
  466.1 4.5 all-to-all-start.11
  470.6 46.7 %all-to-all-done.11 = bf16[8,8,128,128]{3,2,1,0:T(8,128)(2,1)} async-done(((bf16[8,8,128,128]{3,2,1,0:T(8,128)(2,1)}), bf16[8,8,128,128]{3,2,1,0:T(8,128)(2,1)}, u32[]{:S(2)}, u32[]{:S(2)}) %all-to-all-start.11) | async-done | bytes 2097184 | tf_op jit(solution)/shard_map/all_to_all | solution.py:28
  517.3 3.1 copy.29
  520.4 4.1 copy.30
  524.5 3.0 fusion.71
  (91 shorter events, 17.8 us)
Async XLA Ops:
  0.0 99.3 %copy-start = (bf16[1,1,8192,128]{3,2,1,0:T(8,128)(2,1)S(1)}, bf16[1,1,8192,128]{3,2,1,0:T(8,128)(2,1)}, u32[]{:S(2)}) copy-start(bf16[1,1,8192,128]{3,2,1,0:T(8,128)(2,1)} %param.9) | copy-start | bytes 6291460
  33.6 4.7 copy-start.3
  33.7 4.7 copy-start.4
  33.7 49.3 %all-to-all-start.1 = ((bf16[8,8,128,128]{3,2,1,0:T(8,128)(2,1)}), bf16[8,8,128,128]{3,2,1,0:T(8,128)(2,1)}, u32[]{:S(2)}, u32[]{:S(2)}) async-start(bf16[8,8,128,128]{3,2,1,0:T(8,128)(2,1)} %stack.73), calls=%async_computation.1 | async-start | bytes 4194304 | tf_op jit(solution)/shard_map/all_to_all | solution.py:28
  88.9 4.2 copy-start.1
  95.1 3.8 collective-permute-start
  98.9 4.9 collective-permute-start.1
  103.8 7.9 %collective-permute-start.2 = (bf16[128,128]{0,1:T(8,128)(2,1)S(1)}, bf16[128,128]{0,1:T(8,128)(2,1)S(1)}, u32[]{:S(2)}, u32[]{:S(2)}) collective-permute-start(bf16[128,128]{0,1:T(8,128)(2,1)S(1)} %maximum_select_fusion.3), channel_id=1, source_target_pairs={{0,4},{1,5},{2,6},{3,7},{4,0},{5,1},{6,2},{7,3},{8,12},{9,13},{10,... | collective-permute-start | bytes 98312 | tf_op jit(solution)/shard_map/ppermute | solution.py:41
  179.2 5.2 copy-start.2
  182.3 2.2 collective-permute-start.3
  262.3 4.0 collective-permute-start.4
  266.2 4.9 collective-permute-start.5
  271.2 8.0 %collective-permute-start.6 = (bf16[128,128]{0,1:T(8,128)(2,1)S(1)}, bf16[128,128]{0,1:T(8,128)(2,1)S(1)}, u32[]{:S(2)}, u32[]{:S(2)}) collective-permute-start(bf16[128,128]{0,1:T(8,128)(2,1)S(1)} %maximum_select_fusion.4), channel_id=1, source_target_pairs={{0,4},{1,5},{2,6},{3,7},{4,0},{5,1},{6,2},{7,3},{8,12},{9,13},{10,... | collective-permute-start | bytes 98312 | tf_op jit(solution)/shard_map/ppermute | solution.py:41
  352.5 2.2 collective-permute-start.7
  432.5 3.8 collective-permute-start.8
  436.3 4.9 collective-permute-start.9
  441.2 8.0 %collective-permute-start.10 = (bf16[128,128]{0,1:T(8,128)(2,1)S(1)}, bf16[128,128]{0,1:T(8,128)(2,1)S(1)}, u32[]{:S(2)}, u32[]{:S(2)}) collective-permute-start(bf16[128,128]{0,1:T(8,128)(2,1)S(1)} %maximum_select_fusion.5), channel_id=1, source_target_pairs={{0,4},{1,5},{2,6},{3,7},{4,0},{5,1},{6,2},{7,3},{8,12},{9,13},{10,... | collective-permute-start | bytes 98312 | tf_op jit(solution)/shard_map/ppermute | solution.py:41
  466.1 51.2 %all-to-all-start.11 = ((bf16[8,8,128,128]{3,2,1,0:T(8,128)(2,1)}), bf16[8,8,128,128]{3,2,1,0:T(8,128)(2,1)}, u32[]{:S(2)}, u32[]{:S(2)}) async-start(bf16[8,8,128,128]{3,2,1,0:T(8,128)(2,1)} %stack.91), calls=%async_computation.11 | async-start | bytes 4194304 | tf_op jit(solution)/shard_map/all_to_all | solution.py:28
